TPU v7x, 32 devices: a whole 2x2x4 slice. The times are simulated.
32 devices in a mesh: grp: 2 (over x), leaf: 16 (over z, y, core).
Axes of the slice: x: 2, y: 2, z: 4, core: 2. Of those that a mesh axis runs over, the one named last changes fastest.
Arguments:
- points: float32 [8, 32768], P(None, ('grp', 'leaf')), may hold values from -6 to 6
- rhs: float32 [16, 32768], P(None, ('grp', 'leaf')), may hold values from -6 to 6
- basis: float32 [32768, 128], P(('grp', 'leaf')), may hold values from -0.1875 to 0.1875
- transfer: float32 [32, 128, 128], P(('grp', 'leaf')), may hold values from -0.5 to 0.5
- noise: float32 [32768], P(('grp', 'leaf')), may hold values from 0.5 to 2
- inv_scale: float32 [8], replicated, may hold values from 0.15 to 0.6
- links: int32 [32, 2], P(('grp', 'leaf')), may hold values from 0 to 1, as said below
- leaf_skel: int32 [32, 128], P(('grp', 'leaf')), may hold values from 0 to 1023, as said below
- group_skel: int32 [2, 128], P('grp'), may hold values from 0 to 2047, as said below
Outputs:
- solution: float32 [16, 32768], P(None, ('grp', 'leaf'))
- residual: float32 [16, 32768], P(None, ('grp', 'leaf'))
Inputs may be any that keep to these rules, and one draw needn't show every extreme that they name: `links`: column 1 of box l equals column 0 of box l + 1; column 0 is 0 for the first box of each group of 16 and column 1 for the last. `leaf_skel`: the 128 indices of a box are distinct. `group_skel`: the 128 indices of a group are distinct.
All inputs are finite; a program needn't handle non-finite values.
Results may differ from a plain program's by a relative error of at most 0.0003.
Values sent between devices are 32-bit elements; how exact they have to be, the bound alone decides.
No kernel may reach another device: no remote copies, remote signals or barrier semaphores. Data moves between devices by JAX's collectives and lax.ppermute only.
A program may use at most 128 MiB of HBM per device.

v0:
```python
import jax
import jax.numpy as jnp
from jax import lax
from jax.sharding import PartitionSpec as P

ITERS = 2


def padded_2(value, sides, width):
    for axis, dim in sides:
        size, length = (lax.axis_size(axis), value.shape[dim])
        up = [(i, (i + 1) % size) for i in range(size - 1)]
        down = [(j, i) for i, j in up]
        last = lax.slice_in_dim(value, length - width, length, axis=dim)
        initial = lax.slice_in_dim(value, 0, width, axis=dim)
        before = lax.ppermute(last, axis, up)
        after = lax.ppermute(initial, axis, down)
        value = jnp.concatenate([before, value, after], axis=dim)
    return value


def kernel_block(left, right, inv_scale):
    first = left * inv_scale[:, None]
    second = right * inv_scale[:, None]
    cross = lax.dot_general(
        first, second, (((0,), (0,)), ((), ())), precision=lax.Precision.HIGHEST
    )
    dist = (
        jnp.sum(first * first, axis=0)[:, None]
        + jnp.sum(second * second, axis=0)[None, :]
        - 2.0 * cross
    )
    scaled = jnp.sqrt(5.0 * jnp.maximum(dist, 0.0))
    return (1.0 + scaled + scaled * scaled / 3.0) * jnp.exp(-scaled)


def contract(first, second):
    return lax.dot_general(first, second, (((1,), (1,)), ((), ())), precision=lax.Precision.HIGHEST)


def product(first, second):
    return jnp.dot(first, second, precision=lax.Precision.HIGHEST)


def two_products(residual, image):
    return lax.psum(
        (jnp.sum(residual * residual, axis=1), jnp.sum(residual * image, axis=1)), ("grp", "leaf")
    )


def local(points, rhs, basis, transfer, noise, inv_scale, links, leaf_skel, group_skel):
    width = points.shape[1]
    left_bit = links[0, 0]
    right_bit = links[0, 1]
    weight_self = 1.0 + (left_bit + right_bit).astype(jnp.float32)
    skel_pts = points[:, leaf_skel[0]]
    group_pts = lax.all_gather(skel_pts, "leaf", axis=1, tiled=True)
    top_pts = group_pts[:, group_skel[0]]
    top_all = lax.all_gather(top_pts, "grp", axis=1, tiled=True)
    kernel_top = kernel_block(top_pts, top_all, inv_scale)
    kernel_far = kernel_block(skel_pts, group_pts, inv_scale)
    kernel_self = kernel_block(points, points, inv_scale)
    square_zero = jnp.zeros((width, width), jnp.float32)
    lift = transfer[0]
    beside_all = padded_2(points, (("leaf", 1),), width)
    kernel_left = lax.cond(
        left_bit > 0,
        lambda: kernel_block(beside_all[:, :width], points, inv_scale),
        lambda: square_zero,
    )
    kernel_right = lax.cond(
        right_bit > 0,
        lambda: kernel_block(beside_all[:, 2 * width :], points, inv_scale),
        lambda: square_zero,
    )

    def near_part(vec):
        padded = padded_2(vec, (("leaf", 1),), width)
        result = weight_self * product(vec, kernel_self)
        result = result + product(padded[:, :width], kernel_left)
        return result + product(padded[:, 2 * width :], kernel_right)

    def apply(vec):
        coeff = product(vec, basis)
        far = contract(lax.all_gather(coeff, "leaf", axis=1, tiled=True), kernel_far)
        group_coeff = lax.psum(product(coeff, lift), "leaf")
        top_coeff = lax.all_gather(group_coeff, "grp", axis=1, tiled=True)
        top = contract(top_coeff, kernel_top)
        row = far + contract(top, lift)
        return noise[None, :] * vec + near_part(vec) + contract(row, basis)

    solution = jnp.zeros_like(rhs)
    residual = rhs
    image = apply(residual)
    norm_now, curve = two_products(residual, image)
    alpha = norm_now / curve
    direction, along = (residual, image)
    for step in range(ITERS):
        solution = solution + alpha[:, None] * direction
        residual = residual - alpha[:, None] * along
        if step + 1 < ITERS:
            image = apply(residual)
            norm_next, curve = two_products(residual, image)
            ratio = norm_next / norm_now
            alpha = norm_next / (curve - ratio * norm_next / alpha)
            direction = residual + ratio[:, None] * direction
            along = image + ratio[:, None] * along
            norm_now = norm_next
    return (solution, residual)


def solution(mesh):
    return jax.shard_map(
        local,
        mesh=mesh,
        in_specs=(
            P(None, ("grp", "leaf")),
            P(None, ("grp", "leaf")),
            P(("grp", "leaf"), None),
            P(("grp", "leaf"), None, None),
            P(("grp", "leaf")),
            P(),
            P(("grp", "leaf"), None),
            P(("grp", "leaf"), None),
            P("grp", None),
        ),
        out_specs=(P(None, ("grp", "leaf")), P(None, ("grp", "leaf"))),
        check_vma=False,
    )
```

profile of v0, /device:TPU:10, one launch (start us, length us, event | category | flops | bytes accessed | tf_op | source)
XLA Modules:
  0.0 289.5 jit_solution(12969170760022450725)
XLA Ops:
  0.6 2.9 collective-permute-start.2
  3.5 1.9 collective-permute-start
  5.5 4.5 %collective-permute-start.3 = (f32[16,1024]{1,0:T(8,128)}, f32[16,1024]{1,0:T(8,128)S(1)}, u32[]{:S(2)}, u32[]{:S(2)}) collective-permute-start(f32[16,1024]{1,0:T(8,128)} %param.14), channel_id=1, source_target_pairs={{1,0},{2,1},{3,2},{4,3},{5,4},{6,5},{7,6},{8,7},{9,8},{10,9},{11,1... | collective-permute-start | bytes 196616 | tf_op jit(solution)/shard_map/ppermute | solution.py:17
  10.0 1.9 collective-permute-start.1
  14.2 1.3 fusion.39
  17.7 1.2 fusion.41
  18.9 17.5 %all_gather.18 = f32[16,2048]{1,0:T(8,128)S(1)} all-gather(f32[16,128]{1,0:T(8,128)S(1)} %fusion.41), channel_id=1, replica_groups=mesh['grp'=2,'leaf'=16] {'leaf'}, dimensions={1}, use_global_device_ids=true | all-gather | bytes 139264 | tf_op jit(solution)/shard_map/all_gather | solution.py:85
  36.4 1.0 fusion.26
  37.4 25.1 %psum.43 = f32[16,128]{1,0:T(8,128)S(1)} all-reduce(f32[16,128]{1,0:T(8,128)S(1)} %fusion.26), channel_id=1, replica_groups=mesh['grp'=2,'leaf'=16] {'leaf'}, use_global_device_ids=true, to_apply=%region_13.14 | all-reduce | flops 2048 | bytes 16384 | tf_op jit(solution)/shard_map/psum | solution.py:86
  62.5 4.4 %all_gather.20 = f32[16,256]{1,0:T(8,128)S(1)} all-gather(f32[16,128]{1,0:T(8,128)S(1)} %psum.43), channel_id=1, replica_groups=mesh['grp'=2,'leaf'=16] {'grp'}, dimensions={1}, use_global_device_ids=true | all-gather | bytes 24576 | tf_op jit(solution)/shard_map/all_gather | solution.py:87
  67.5 25.8 %all-gather = f32[8,2048]{0,1:T(8,128)S(1)} all-gather(f32[8,128]{0,1:T(8,128)S(1)} %bitcast.71), channel_id=2, replica_groups=mesh['grp'=2,'leaf'=16] {'leaf'}, dimensions={1}, use_global_device_ids=true | all-gather | bytes 69632 | tf_op jit(solution)/shard_map/all_gather | solution.py:57
  93.2 1.0 multiply_reduce_fusion.4
  95.7 5.0 %all-gather.1 = f32[8,256]{0,1:T(8,128)S(1)} all-gather(f32[8,128]{0,1:T(8,128)S(1)} %bitcast.70), channel_id=3, replica_groups=mesh['grp'=2,'leaf'=16] {'grp'}, dimensions={1}, use_global_device_ids=true | all-gather | bytes 12288 | tf_op jit(solution)/shard_map/all_gather | solution.py:59
  101.5 6.9 %exponential_multiply_fusion.2 = f32[1024,1024]{1,0:T(8,128)S(1)} fusion(f32[1024]{0:T(1024)S(1)} %multiply_reduce_fusion.12, f32[8,1024]{1,0:T(8,128)} %param.13, f32[8]{0:T(128)} %param.18), kind=kOutput, calls=%fused_computation.14 | convolution fusion | flops 112205824 | bytes 4231200 | tf_op jit(solution)/shard_map/dot_general | solution.py:25
  108.4 1.6 exponential_multiply_fusion.3
  111.7 2.3 convolution_multiply_fusion.3
  115.9 2.5 conditional.2
  115.9 2.5 broadcast.88
  118.4 2.5 conditional.3
  118.4 2.5 broadcast.94
  120.9 4.6 %fusion.40 = f32[1024,16]{0,1:T(8,128)S(1)} fusion(f32[1024,1024]{1,0:T(8,128)} %get-tuple-element.49, f32[16,1024]{1,0:T(8,128)S(1)} %collective-permute-done.3), kind=kOutput, calls=%fused_computation.77 | convolution fusion | flops 201326592 | bytes 4325376 | tf_op jit(solution)/shard_map/dot_general | solution.py:42
  125.6 2.4 multiply_reduce_fusion.8
  128.0 49.4 %all-reduce.1 = (f32[16]{0:T(128)S(1)}, f32[16]{0:T(128)S(1)}) all-reduce(f32[16]{0:T(128)S(1)} %get-tuple-element.33, f32[16]{0:T(128)S(1)} %get-tuple-element.32), channel_id=1, replica_groups=mesh['grp'=2,'leaf'=16] {'grp','leaf'}, use_global_device_ids=true, to_apply=%region_1.0 | all-reduce | flops 32 | bytes 256 | tf_op jit(solution)/shard_map/psum | solution.py:46
  177.4 4.3 %convolution_multiply_fusion.2 = f32[16,1024]{1,0:T(8,128)S(1)} fusion(f32[16,1024]{1,0:T(8,128)S(1)} %multiply_subtract_fusion.1, f32[1024,1024]{1,0:T(8,128)} %copy-done.3, f32[]{:T(128)} %bitcast), kind=kOutput, calls=%fused_computation.26 | convolution fusion | flops 201342976 | bytes 4325380 | tf_op jit(solution)/shard_map/dot_general | solution.py:42
  182.1 1.9 collective-permute-start.5
  184.0 2.4 collective-permute-start.4
  186.6 16.7 %all_gather.22 = f32[16,2048]{1,0:T(8,128)S(1)} all-gather(f32[16,128]{1,0:T(8,128)S(1)} %fusion.46), channel_id=1, replica_groups=mesh['grp'=2,'leaf'=16] {'leaf'}, dimensions={1}, use_global_device_ids=true | all-gather | bytes 139264 | tf_op jit(solution)/shard_map/all_gather | solution.py:85
  203.3 25.0 %psum.46 = f32[16,128]{1,0:T(8,128)S(1)} all-reduce(f32[16,128]{1,0:T(8,128)S(1)} %fusion.23), channel_id=1, replica_groups=mesh['grp'=2,'leaf'=16] {'leaf'}, use_global_device_ids=true, to_apply=%region_20.0 | all-reduce | flops 2048 | bytes 16384 | tf_op jit(solution)/shard_map/psum | solution.py:86
  228.3 4.5 %all_gather.23 = f32[16,256]{1,0:T(8,128)S(1)} all-gather(f32[16,128]{1,0:T(8,128)S(1)} %psum.46), channel_id=1, replica_groups=mesh['grp'=2,'leaf'=16] {'grp'}, dimensions={1}, use_global_device_ids=true | all-gather | bytes 24576 | tf_op jit(solution)/shard_map/all_gather | solution.py:87
  234.2 4.3 %fusion.45 = f32[16,1024]{1,0:T(8,128)S(1)} fusion(f32[16,1024]{1,0:T(8,128)S(1)} %collective-permute-done.5, f32[1024,1024]{1,0:T(8,128)} %get-tuple-element.49), kind=kOutput, calls=%fused_computation.82 | convolution fusion | flops 201326592 | bytes 4325376 | tf_op jit(solution)/shard_map/dot_general | solution.py:42
  238.5 2.1 fusion.18
  241.2 47.5 %all-reduce = (f32[16]{0:T(128)S(1)}, f32[16]{0:T(128)S(1)}) all-reduce(f32[16]{0:T(128)S(1)} %get-tuple-element.31, f32[16]{0:T(128)S(1)} %get-tuple-element.30), channel_id=1, replica_groups=mesh['grp'=2,'leaf'=16] {'grp','leaf'}, use_global_device_ids=true, to_apply=%region_19.0 | all-reduce | flops 32 | bytes 256 | tf_op jit(solution)/shard_map/psum | solution.py:46
  (49 shorter events, 11.6 us)
Async XLA Ops:
  0.6 17.1 %copy-start = (f32[1024,128]{1,0:T(8,128)S(1)}, f32[1024,128]{1,0:T(8,128)}, u32[]{:S(2)}) copy-start(f32[1024,128]{1,0:T(8,128)} %param.15) | copy-start | bytes 1572868
  0.6 117.8 %collective-permute-start.2 = (f32[8,1024]{1,0:T(8,128)}, f32[8,1024]{1,0:T(8,128)S(1)}, u32[]{:S(2)}, u32[]{:S(2)}) collective-permute-start(f32[8,1024]{1,0:T(8,128)} %param.13), channel_id=1, source_target_pairs={{1,0},{2,1},{3,2},{4,3},{5,4},{6,5},{7,6},{8,7},{9,8},{10,9},{11,1... | collective-permute-start | bytes 98312 | tf_op jit(solution)/shard_map/ppermute | solution.py:17
  3.5 112.4 %collective-permute-start = (f32[8,1024]{1,0:T(8,128)}, f32[8,1024]{1,0:T(8,128)S(1)}, u32[]{:S(2)}, u32[]{:S(2)}) collective-permute-start(f32[8,1024]{1,0:T(8,128)} %param.13), channel_id=1, source_target_pairs={{0,1},{1,2},{2,3},{3,4},{4,5},{5,6},{6,7},{7,8},{8,9},{9,10},{10,1... | collective-permute-start | bytes 98312 | tf_op jit(solution)/shard_map/ppermute | solution.py:16
  5.5 115.5 %collective-permute-start.3 = (f32[16,1024]{1,0:T(8,128)}, f32[16,1024]{1,0:T(8,128)S(1)}, u32[]{:S(2)}, u32[]{:S(2)}) collective-permute-start(f32[16,1024]{1,0:T(8,128)} %param.14), channel_id=1, source_target_pairs={{1,0},{2,1},{3,2},{4,3},{5,4},{6,5},{7,6},{8,7},{9,8},{10,9},{11,1... | collective-permute-start | bytes 196616 | tf_op jit(solution)/shard_map/ppermute | solution.py:17
  10.0 115.5 %collective-permute-start.1 = (f32[16,1024]{1,0:T(8,128)}, f32[16,1024]{1,0:T(8,128)S(1)}, u32[]{:S(2)}, u32[]{:S(2)}) collective-permute-start(f32[16,1024]{1,0:T(8,128)} %param.14), channel_id=1, source_target_pairs={{0,1},{1,2},{2,3},{3,4},{4,5},{5,6},{6,7},{7,8},{8,9},{9,10},{10,1... | collective-permute-start | bytes 196616 | tf_op jit(solution)/shard_map/ppermute | solution.py:16
  101.5 6.9 %copy-start.8 = (f32[8]{0:T(128)S(1)}, f32[8]{0:T(128)}, u32[]{:S(2)}) copy-start(f32[8]{0:T(128)} %param.18) | copy-start | bytes 100
  108.3 5.7 %copy-start.3 = (f32[1024,1024]{1,0:T(8,128)}, f32[1024,1024]{1,0:T(8,128)S(1)}, u32[]{:S(2)}) copy-start(f32[1024,1024]{1,0:T(8,128)S(1)} %exponential_multiply_fusion.2) | copy-start | bytes 12582916
  108.3 3.1 %copy-start.5 = (f32[1,128,128]{2,1,0:T(8,128)S(1)}, f32[1,128,128]{2,1,0:T(8,128)}, u32[]{:S(2)}) copy-start(f32[1,128,128]{2,1,0:T(8,128)} %param.16) | copy-start | bytes 196612
  108.4 3.4 %copy-start.4 = (f32[16,1024]{1,0:T(8,128)S(1)}, f32[16,1024]{1,0:T(8,128)}, u32[]{:S(2)}) copy-start(f32[16,1024]{1,0:T(8,128)} %param.14) | copy-start | bytes 196612
  110.0 5.9 %copy-start.6 = (f32[8,1024]{1,0:T(8,128)S(1)}, f32[8,1024]{1,0:T(8,128)}, u32[]{:S(2)}) copy-start(f32[8,1024]{1,0:T(8,128)} %param.13) | copy-start | bytes 98308
  120.9 4.6 %copy-start.7 = (f32[1024]{0:T(1024)S(1)}, f32[1024]{0:T(1024)}, u32[]{:S(2)}) copy-start(f32[1024]{0:T(1024)} %param.17) | copy-start | bytes 12292
  120.9 4.6 %copy-start.1 = (f32[1024,1024]{1,0:T(8,128)S(1)}, f32[1024,1024]{1,0:T(8,128)}, u32[]{:S(2)}) copy-start(f32[1024,1024]{1,0:T(8,128)} %get-tuple-element.48) | copy-start | bytes 12582916
  182.1 52.1 %collective-permute-start.5 = (f32[16,1024]{1,0:T(8,128)S(1)}, f32[16,1024]{1,0:T(8,128)S(1)}, u32[]{:S(2)}, u32[]{:S(2)}) collective-permute-start(f32[16,1024]{1,0:T(8,128)S(1)} %multiply_subtract_fusion.1), channel_id=1, source_target_pairs={{1,0},{2,1},{3,2},{4,3},{5,4},{6,5},{7,6},{8,7},{9,8},{10,9},{11,1... | collective-permute-start | bytes 196616 | tf_op jit(solution)/shard_map/ppermute | solution.py:17
  184.0 54.5 %collective-permute-start.4 = (f32[16,1024]{1,0:T(8,128)S(1)}, f32[16,1024]{1,0:T(8,128)S(1)}, u32[]{:S(2)}, u32[]{:S(2)}) collective-permute-start(f32[16,1024]{1,0:T(8,128)S(1)} %multiply_subtract_fusion.1), channel_id=1, source_target_pairs={{0,1},{1,2},{2,3},{3,4},{4,5},{5,6},{6,7},{7,8},{8,9},{9,10},{10,1... | collective-permute-start | bytes 196616 | tf_op jit(solution)/shard_map/ppermute | solution.py:16
  228.3 10.2 %copy-start.2 = (f32[1024,1024]{1,0:T(8,128)S(1)}, f32[1024,1024]{1,0:T(8,128)}, u32[]{:S(2)}) copy-start(f32[1024,1024]{1,0:T(8,128)} %get-tuple-element.48) | copy-start | bytes 12582916
where the time goes:
time: 290 us
  blocking collectives  221 us (76%)
  matrix products  35.3 us (12%)
  starting transfers between devices  15.6 us (5%)
  local copies, waits for them, and re-layouts  8.64 us (3%)
  other arithmetic  5.55 us (2%)
  between operations  3.6 us (1%)
    psum x2, blocking collectives, two_products(): lax.psum((jnp.sum(residual * residual, axis=1), jnp.sum(residual * image,...  96.9 us
    psum x2, blocking collectives, apply(): group_coeff = lax.psum(product(coeff, lift), 'leaf')  50.1 us
    all_gather x2, blocking collectives, apply(): lax.all_gather(coeff, 'leaf', axis=1, tiled=True)  34.1 us
    all_gather x1, blocking collectives, local(): group_pts = lax.all_gather(skel_pts, 'leaf', axis=1, tiled=True)  25.8 us
    dot_general x10, matrix products, product(): return jnp.dot(first, second, precision=lax.Precision.HIGHEST)  22.7 us
    ppermute x3, starting transfers between devices, padded_2(): after = lax.ppermute(initial, axis, down)  9.35 us
    all_gather x2, blocking collectives, apply(): top_coeff = lax.all_gather(group_coeff, 'grp', axis=1, tiled=True)  8.85 us
    dot_general x3, matrix products, kernel_block(): lax.dot_general(first, second, (((0,), (0,)), ((), ())), precision=lax.Pr...  8.84 us
  transfers between devices with their start and end apart: 6, of which 0 were waited for; matrix products, arithmetic and copies ran while one was open for 13% of the time, Pallas kernels for 0%

commit v1 on v0

--- a/solution.py
+++ b/solution.py
@@ -83,7 +83,7 @@
     def apply(vec):
         coeff = product(vec, basis)
         far = contract(lax.all_gather(coeff, "leaf", axis=1, tiled=True), kernel_far)
-        group_coeff = lax.psum(product(coeff, lift), "leaf")
+        group_coeff = jnp.sum(lax.all_gather(product(coeff, lift), "leaf"), axis=0)
         top_coeff = lax.all_gather(group_coeff, "grp", axis=1, tiled=True)
         top = contract(top_coeff, kernel_top)
         row = far + contract(top, lift)

time: 290 us -> 267 us (0.921)
  blocking collectives: 221 us -> 199 us
    psum x2 -> x0, blocking collectives: 50.1 us -> none  [apply(): group_coeff = lax.psum(product(coeff, lift), 'leaf')]
    all_gather x0 -> x2, blocking collectives: none -> 35.6 us  [apply(): group_coeff = jnp.sum(lax.all_gather(product(coeff, lift), 'leaf'), axis=0)]
    psum x2, blocking collectives: 96.9 us -> 92.8 us  [two_products(): lax.psum((jnp.sum(residual * residual, axis=1), jnp.sum(residual * image,...]
    all_gather x1, blocking collectives: 25.8 us -> 21.8 us  [local(): group_pts = lax.all_gather(skel_pts, 'leaf', axis=1, tiled=True)]
  transfers between devices with their start and end apart: 6 -> 6, of which waited for: 0 -> 0; matrix products, arithmetic and copies ran while one was open for 13% -> 14% of each run, Pallas kernels for 0% -> 0%
where the time goes in v1:
time: 267 us; the launch traced here: 266 us
  blocking collectives  199 us (75%)
  matrix products  34.4 us (13%)
  starting transfers between devices  15.6 us (6%)
  local copies, waits for them, and re-layouts  8.64 us (3%)
  other arithmetic  4.93 us (2%)
  between operations  3.58 us (1%)
    psum x2, blocking collectives, two_products(): lax.psum((jnp.sum(residual * residual, axis=1), jnp.sum(residual * image,...  92.8 us
    all_gather x2, blocking collectives, apply(): group_coeff = jnp.sum(lax.all_gather(product(coeff, lift), 'leaf'), axis=0)  35.6 us
    all_gather x2, blocking collectives, apply(): lax.all_gather(coeff, 'leaf', axis=1, tiled=True)  34.6 us
    dot_general x10, matrix products, product(): return jnp.dot(first, second, precision=lax.Precision.HIGHEST)  22.7 us
    all_gather x1, blocking collectives, local(): group_pts = lax.all_gather(skel_pts, 'leaf', axis=1, tiled=True)  21.8 us
    ppermute x3, starting transfers between devices, padded_2(): after = lax.ppermute(initial, axis, down)  9.35 us
    all_gather x2, blocking collectives, apply(): top_coeff = lax.all_gather(group_coeff, 'grp', axis=1, tiled=True)  8.85 us
    dot_general x3, matrix products, kernel_block(): lax.dot_general(first, second, (((0,), (0,)), ((), ())), precision=lax.Pr...  8 us
  transfers between devices with their start and end apart: 6, of which 0 were waited for; matrix products, arithmetic and copies ran while one was open for 14% of the time, Pallas kernels for 0%

profile of v1, /device:TPU:10, one launch (start us, length us, event | category | flops | bytes accessed | tf_op | source)
XLA Modules:
  0.0 265.9 jit_solution(65771734738916759)
XLA Ops:
  0.7 2.9 %collective-permute-start.2 = (f32[8,1024]{1,0:T(8,128)}, f32[8,1024]{1,0:T(8,128)S(1)}, u32[]{:S(2)}, u32[]{:S(2)}) collective-permute-start(f32[8,1024]{1,0:T(8,128)} %param.13), channel_id=1, source_target_pairs={{1,0},{2,1},{3,2},{4,3},{5,4},{6,5},{7,6},{8,7},{9,8},{10,9},{11,1... | collective-permute-start | bytes 98312 | tf_op jit(solution)/shard_map/ppermute | solution.py:17
  3.6 1.9 collective-permute-start
  5.5 4.5 %collective-permute-start.3 = (f32[16,1024]{1,0:T(8,128)}, f32[16,1024]{1,0:T(8,128)S(1)}, u32[]{:S(2)}, u32[]{:S(2)}) collective-permute-start(f32[16,1024]{1,0:T(8,128)} %param.14), channel_id=1, source_target_pairs={{1,0},{2,1},{3,2},{4,3},{5,4},{6,5},{7,6},{8,7},{9,8},{10,9},{11,1... | collective-permute-start | bytes 196616 | tf_op jit(solution)/shard_map/ppermute | solution.py:17
  10.0 1.9 collective-permute-start.1
  14.3 1.3 fusion.39
  17.8 1.2 fusion.41
  19.0 17.5 %all_gather.30 = f32[16,2048]{1,0:T(8,128)S(1)} all-gather(f32[16,128]{1,0:T(8,128)S(1)} %fusion.41), channel_id=1, replica_groups=mesh['grp'=2,'leaf'=16] {'leaf'}, dimensions={1}, use_global_device_ids=true | all-gather | bytes 139264 | tf_op jit(solution)/shard_map/all_gather | solution.py:85
  36.4 1.0 fusion.26
  37.4 17.8 %all-gather.1 = f32[256,128]{1,0:T(8,128)S(1)} all-gather(f32[16,128]{1,0:T(8,128)S(1)} %fusion.26), channel_id=3, replica_groups=mesh['grp'=2,'leaf'=16] {'leaf'}, dimensions={0}, use_global_device_ids=true | all-gather | bytes 139264 | tf_op jit(solution)/shard_map/all_gather | solution.py:86
  55.2 4.4 %all_gather.34 = f32[16,256]{1,0:T(8,128)S(1)} all-gather(f32[16,128]{1,0:T(8,128)S(1)} %reduce_sum.143), channel_id=1, replica_groups=mesh['grp'=2,'leaf'=16] {'grp'}, dimensions={1}, use_global_device_ids=true | all-gather | bytes 24576 | tf_op jit(solution)/shard_map/all_gather | solution.py:87
  60.2 21.8 %all-gather = f32[8,2048]{0,1:T(8,128)S(1)} all-gather(f32[8,128]{0,1:T(8,128)S(1)} %bitcast.75), channel_id=2, replica_groups=mesh['grp'=2,'leaf'=16] {'leaf'}, dimensions={1}, use_global_device_ids=true | all-gather | bytes 69632 | tf_op jit(solution)/shard_map/all_gather | solution.py:57
  82.1 1.0 multiply_reduce_fusion.4
  84.5 5.0 %all-gather.2 = f32[8,256]{0,1:T(8,128)S(1)} all-gather(f32[8,128]{0,1:T(8,128)S(1)} %bitcast.74), channel_id=4, replica_groups=mesh['grp'=2,'leaf'=16] {'grp'}, dimensions={1}, use_global_device_ids=true | all-gather | bytes 12288 | tf_op jit(solution)/shard_map/all_gather | solution.py:59
  89.6 6.0 %exponential_multiply_fusion.2 = f32[1024,1024]{1,0:T(8,128)S(1)} fusion(f32[1024]{0:T(1024)S(1)} %multiply_reduce_fusion.12, f32[8,1024]{1,0:T(8,128)S(1)} %copy-done.6, f32[8]{0:T(128)S(1)} %copy-done.8), kind=kOutput, calls=%fused_computation.14 | convolution fusion | flops 112205824 | bytes 4231200 | tf_op jit(solution)/shard_map/dot_general | solution.py:25
  95.7 1.6 exponential_multiply_fusion.3
  99.1 2.3 convolution_multiply_fusion.3
  103.2 2.5 conditional.2
  103.2 2.5 broadcast.88
  105.7 2.5 conditional.3
  105.7 2.5 broadcast.94
  108.2 4.6 %fusion.40 = f32[1024,16]{0,1:T(8,128)S(1)} fusion(f32[1024,1024]{1,0:T(8,128)} %get-tuple-element.49, f32[16,1024]{1,0:T(8,128)S(1)} %collective-permute-done.3), kind=kOutput, calls=%fused_computation.77 | convolution fusion | flops 201326592 | bytes 4325376 | tf_op jit(solution)/shard_map/dot_general | solution.py:42
  112.9 2.4 multiply_reduce_fusion.8
  115.3 49.8 %all-reduce.1 = (f32[16]{0:T(128)S(1)}, f32[16]{0:T(128)S(1)}) all-reduce(f32[16]{0:T(128)S(1)} %get-tuple-element.33, f32[16]{0:T(128)S(1)} %get-tuple-element.32), channel_id=1, replica_groups=mesh['grp'=2,'leaf'=16] {'grp','leaf'}, use_global_device_ids=true, to_apply=%region_1.0 | all-reduce | flops 32 | bytes 256 | tf_op jit(solution)/shard_map/psum | solution.py:46
  165.1 4.3 %convolution_multiply_fusion.2 = f32[16,1024]{1,0:T(8,128)S(1)} fusion(f32[16,1024]{1,0:T(8,128)S(1)} %multiply_subtract_fusion.1, f32[1024,1024]{1,0:T(8,128)} %copy-done.3, f32[]{:T(128)} %bitcast), kind=kOutput, calls=%fused_computation.26 | convolution fusion | flops 201342976 | bytes 4325380 | tf_op jit(solution)/shard_map/dot_general | solution.py:42
  169.8 1.9 collective-permute-start.5
  171.7 2.4 collective-permute-start.4
  174.3 17.1 %all_gather.36 = f32[16,2048]{1,0:T(8,128)S(1)} all-gather(f32[16,128]{1,0:T(8,128)S(1)} %fusion.46), channel_id=1, replica_groups=mesh['grp'=2,'leaf'=16] {'leaf'}, dimensions={1}, use_global_device_ids=true | all-gather | bytes 139264 | tf_op jit(solution)/shard_map/all_gather | solution.py:85
  192.3 17.8 %all-gather.3 = f32[256,128]{1,0:T(8,128)S(1)} all-gather(f32[16,128]{1,0:T(8,128)S(1)} %fusion.23), channel_id=5, replica_groups=mesh['grp'=2,'leaf'=16] {'leaf'}, dimensions={0}, use_global_device_ids=true | all-gather | bytes 139264 | tf_op jit(solution)/shard_map/all_gather | solution.py:86
  210.2 4.5 %all_gather.39 = f32[16,256]{1,0:T(8,128)S(1)} all-gather(f32[16,128]{1,0:T(8,128)S(1)} %reduce_sum.148), channel_id=1, replica_groups=mesh['grp'=2,'leaf'=16] {'grp'}, dimensions={1}, use_global_device_ids=true | all-gather | bytes 24576 | tf_op jit(solution)/shard_map/all_gather | solution.py:87
  215.1 4.3 %fusion.45 = f32[16,1024]{1,0:T(8,128)S(1)} fusion(f32[16,1024]{1,0:T(8,128)S(1)} %collective-permute-done.5, f32[1024,1024]{1,0:T(8,128)} %get-tuple-element.49), kind=kOutput, calls=%fused_computation.82 | convolution fusion | flops 201326592 | bytes 4325376 | tf_op jit(solution)/shard_map/dot_general | solution.py:42
  219.4 2.1 fusion.18
  222.1 43.0 %all-reduce = (f32[16]{0:T(128)S(1)}, f32[16]{0:T(128)S(1)}) all-reduce(f32[16]{0:T(128)S(1)} %get-tuple-element.31, f32[16]{0:T(128)S(1)} %get-tuple-element.30), channel_id=1, replica_groups=mesh['grp'=2,'leaf'=16] {'grp','leaf'}, use_global_device_ids=true, to_apply=%region_19.0 | all-reduce | flops 32 | bytes 256 | tf_op jit(solution)/shard_map/psum | solution.py:46
  (51 shorter events, 10.9 us)
Async XLA Ops:
  0.6 17.1 %copy-start = (f32[1024,128]{1,0:T(8,128)S(1)}, f32[1024,128]{1,0:T(8,128)}, u32[]{:S(2)}) copy-start(f32[1024,128]{1,0:T(8,128)} %param.15) | copy-start | bytes 1572868
  0.6 89.0 %copy-start.6 = (f32[8,1024]{1,0:T(8,128)S(1)}, f32[8,1024]{1,0:T(8,128)}, u32[]{:S(2)}) copy-start(f32[8,1024]{1,0:T(8,128)} %param.13) | copy-start | bytes 98308
  0.7 88.8 %copy-start.8 = (f32[8]{0:T(128)S(1)}, f32[8]{0:T(128)}, u32[]{:S(2)}) copy-start(f32[8]{0:T(128)} %param.18) | copy-start | bytes 100
  0.7 105.1 %collective-permute-start.2 = (f32[8,1024]{1,0:T(8,128)}, f32[8,1024]{1,0:T(8,128)S(1)}, u32[]{:S(2)}, u32[]{:S(2)}) collective-permute-start(f32[8,1024]{1,0:T(8,128)} %param.13), channel_id=1, source_target_pairs={{1,0},{2,1},{3,2},{4,3},{5,4},{6,5},{7,6},{8,7},{9,8},{10,9},{11,1... | collective-permute-start | bytes 98312 | tf_op jit(solution)/shard_map/ppermute | solution.py:17
  3.6 99.6 %collective-permute-start = (f32[8,1024]{1,0:T(8,128)}, f32[8,1024]{1,0:T(8,128)S(1)}, u32[]{:S(2)}, u32[]{:S(2)}) collective-permute-start(f32[8,1024]{1,0:T(8,128)} %param.13), channel_id=1, source_target_pairs={{0,1},{1,2},{2,3},{3,4},{4,5},{5,6},{6,7},{7,8},{8,9},{9,10},{10,1... | collective-permute-start | bytes 98312 | tf_op jit(solution)/shard_map/ppermute | solution.py:16
  5.5 102.7 %collective-permute-start.3 = (f32[16,1024]{1,0:T(8,128)}, f32[16,1024]{1,0:T(8,128)S(1)}, u32[]{:S(2)}, u32[]{:S(2)}) collective-permute-start(f32[16,1024]{1,0:T(8,128)} %param.14), channel_id=1, source_target_pairs={{1,0},{2,1},{3,2},{4,3},{5,4},{6,5},{7,6},{8,7},{9,8},{10,9},{11,1... | collective-permute-start | bytes 196616 | tf_op jit(solution)/shard_map/ppermute | solution.py:17
  10.0 102.8 %collective-permute-start.1 = (f32[16,1024]{1,0:T(8,128)}, f32[16,1024]{1,0:T(8,128)S(1)}, u32[]{:S(2)}, u32[]{:S(2)}) collective-permute-start(f32[16,1024]{1,0:T(8,128)} %param.14), channel_id=1, source_target_pairs={{0,1},{1,2},{2,3},{3,4},{4,5},{5,6},{6,7},{7,8},{8,9},{9,10},{10,1... | collective-permute-start | bytes 196616 | tf_op jit(solution)/shard_map/ppermute | solution.py:16
  95.7 5.7 %copy-start.3 = (f32[1024,1024]{1,0:T(8,128)}, f32[1024,1024]{1,0:T(8,128)S(1)}, u32[]{:S(2)}) copy-start(f32[1024,1024]{1,0:T(8,128)S(1)} %exponential_multiply_fusion.2) | copy-start | bytes 12582916
  95.7 3.1 %copy-start.5 = (f32[1,128,128]{2,1,0:T(8,128)S(1)}, f32[1,128,128]{2,1,0:T(8,128)}, u32[]{:S(2)}) copy-start(f32[1,128,128]{2,1,0:T(8,128)} %param.16) | copy-start | bytes 196612
  95.7 3.3 %copy-start.4 = (f32[16,1024]{1,0:T(8,128)S(1)}, f32[16,1024]{1,0:T(8,128)}, u32[]{:S(2)}) copy-start(f32[16,1024]{1,0:T(8,128)} %param.14) | copy-start | bytes 196612
  108.2 4.6 %copy-start.7 = (f32[1024]{0:T(1024)S(1)}, f32[1024]{0:T(1024)}, u32[]{:S(2)}) copy-start(f32[1024]{0:T(1024)} %param.17) | copy-start | bytes 12292
  108.2 4.6 %copy-start.1 = (f32[1024,1024]{1,0:T(8,128)S(1)}, f32[1024,1024]{1,0:T(8,128)}, u32[]{:S(2)}) copy-start(f32[1024,1024]{1,0:T(8,128)} %get-tuple-element.48) | copy-start | bytes 12582916
  169.8 45.3 %collective-permute-start.5 = (f32[16,1024]{1,0:T(8,128)S(1)}, f32[16,1024]{1,0:T(8,128)S(1)}, u32[]{:S(2)}, u32[]{:S(2)}) collective-permute-start(f32[16,1024]{1,0:T(8,128)S(1)} %multiply_subtract_fusion.1), channel_id=1, source_target_pairs={{1,0},{2,1},{3,2},{4,3},{5,4},{6,5},{7,6},{8,7},{9,8},{10,9},{11,1... | collective-permute-start | bytes 196616 | tf_op jit(solution)/shard_map/ppermute | solution.py:17
  171.7 47.7 %collective-permute-start.4 = (f32[16,1024]{1,0:T(8,128)S(1)}, f32[16,1024]{1,0:T(8,128)S(1)}, u32[]{:S(2)}, u32[]{:S(2)}) collective-permute-start(f32[16,1024]{1,0:T(8,128)S(1)} %multiply_subtract_fusion.1), channel_id=1, source_target_pairs={{0,1},{1,2},{2,3},{3,4},{4,5},{5,6},{6,7},{7,8},{8,9},{9,10},{10,1... | collective-permute-start | bytes 196616 | tf_op jit(solution)/shard_map/ppermute | solution.py:16
  210.2 9.2 %copy-start.2 = (f32[1024,1024]{1,0:T(8,128)S(1)}, f32[1024,1024]{1,0:T(8,128)}, u32[]{:S(2)}) copy-start(f32[1024,1024]{1,0:T(8,128)} %get-tuple-element.48) | copy-start | bytes 12582916
